TPU v7x, 32 devices: a whole 2x2x4 slice. The times are simulated.
32 devices in a mesh: pool: 4 (over z), fft: 8 (over y, x, core).
Axes of the slice: x: 2, y: 2, z: 4, core: 2. Of those that a mesh axis runs over, the one named last changes fastest.
Arguments:
- orbitals: bfloat16 [4, 2, 1, 160, 25600], P('pool', None, None, 'fft'), may hold values from -6 to 6
- stick_map: int32 [16000], replicated, may hold values from -1 to 25599, as said below
- kpoint_grid: int32 [4, 3], replicated, may hold values from 0 to 3, as said below
Outputs:
- exchange_action: bfloat16 [4, 2, 1, 160, 25600], P('pool', None, None, 'fft')
Inputs may be any that keep to these rules, and one draw needn't show every extreme that they name: `stick_map`: entries other than -1 are distinct columns. Slots come in blocks of 2000 per index of fft; in each block at least half of the slots are live, and in every draw some block has all 2000 live. `kpoint_grid`: rows are distinct.
All inputs are finite; a program needn't handle non-finite values.
Results may differ from a plain program's by a relative error of at most 0.011.
Values may be sent and summed in bfloat16 or wider, within the bound.
A program may use at most 64 MiB of HBM per device.

v0:
```python
import math

import jax
import jax.numpy as jnp
from jax import lax
from jax.sharding import PartitionSpec as P

NG = 160
KMESH = 4


SPACING_BOHR = 0.1875
SCREENING = 0.106


def shifted(value, axis, steps):
    count = lax.axis_size(axis)
    pairs = [(source, (source + steps) % count) for source in range(count)]
    return lax.ppermute(value, axis, pairs)


def dft_table(grid_size, orientation):
    positions = jnp.arange(grid_size, dtype=jnp.int32)
    product = positions[:, None] * positions[None, :] % grid_size
    angle = product.astype(jnp.float32) * (2.0 * math.pi / grid_size)
    cosine = jnp.cos(angle)
    sine = orientation * jnp.sin(angle)
    upper = jnp.stack([cosine, sine], axis=1)
    lower = jnp.stack([-sine, cosine], axis=1)
    return jnp.stack([upper, lower], axis=0).astype(jnp.bfloat16)


def signed(frequency, grid_size):
    return jnp.where(frequency >= grid_size // 2, frequency - grid_size, frequency)


def kernel_table(columns, shift_q, grid_size):
    live_slot = columns >= 0
    column_ids = jnp.where(live_slot, columns, 0)
    freq_x = signed(column_ids % grid_size, grid_size)
    freq_y = signed(column_ids // grid_size, grid_size)
    freq_z = signed(jnp.arange(grid_size, dtype=jnp.int32), grid_size)
    radius = grid_size // 2
    inside = (freq_x * freq_x + freq_y * freq_y)[None, :] + (freq_z * freq_z)[
        :, None
    ] <= radius * radius
    inside = jnp.logical_and(inside, live_slot[None, :])
    wave_x = freq_x.astype(jnp.float32) + shift_q[0]
    wave_y = freq_y.astype(jnp.float32) + shift_q[1]
    wave_z = freq_z.astype(jnp.float32) + shift_q[2]
    square = (wave_z * wave_z)[:, None] + (wave_x * wave_x + wave_y * wave_y)[None, :]
    cell = SPACING_BOHR * grid_size
    exponent = math.pi * math.pi * square / (cell * cell * SCREENING * SCREENING)
    weights = cell * cell / math.pi * -jnp.expm1(-exponent) / square / float(grid_size) ** 3
    return jnp.where(inside, weights, 0.0)


def momentum(kpoint_grid, pool_rank, pool_count):
    pool_rows = jnp.arange(pool_count, dtype=jnp.int32)
    earlier = (pool_rank + pool_count - 1) % pool_count
    current = jnp.sum(jnp.where((pool_rows == pool_rank)[:, None], kpoint_grid, 0), axis=0)
    previous = jnp.sum(jnp.where((pool_rows == earlier)[:, None], kpoint_grid, 0), axis=0)
    return (current - previous).astype(jnp.float32) / KMESH


def pair_density(own_bands, received):
    band_count = own_bands.shape[1]
    real_own = own_bands[0].astype(jnp.float32)[:, None]
    imag_own = own_bands[1].astype(jnp.float32)[:, None]
    real_recv = received[0].astype(jnp.float32)[None]
    imag_recv = received[1].astype(jnp.float32)[None]
    real_part = real_recv * real_own + imag_recv * imag_own
    imag_part = real_recv * imag_own - imag_recv * real_own
    stacked = jnp.stack([real_part, imag_part], axis=2)
    return stacked.reshape((band_count * band_count, 2) + own_bands.shape[2:]).astype(jnp.bfloat16)


def action_of(received, field):
    band_count = received.shape[1]
    field = field.reshape((band_count, band_count) + field.shape[1:])
    real_recv = received[0].astype(jnp.float32)[None]
    imag_recv = received[1].astype(jnp.float32)[None]
    real_field = field[:, :, 0]
    imag_field = field[:, :, 1]
    real_part = -jnp.sum(real_recv * real_field - imag_recv * imag_field, axis=1)
    imag_part = -jnp.sum(real_recv * imag_field + imag_recv * real_field, axis=1)
    return jnp.stack([real_part, imag_part], axis=0).astype(jnp.bfloat16)


def apply_table(data, table, form):
    return jnp.einsum(form, data, table, preferred_element_type=jnp.float32)


def column_pass(picked, weights, forward, backward):
    spectrum = apply_table(picked, forward, "pczs,czdk->pdks")
    scaled = (spectrum * weights).astype(jnp.bfloat16)
    return apply_table(scaled, backward, "pczs,czdk->pdks").astype(jnp.bfloat16)


def local(orbitals, stick_map, kpoint_grid):
    grid_size = NG
    moved = shifted(orbitals, "pool", 1)
    own_bands = orbitals[0].reshape(orbitals.shape[1:4] + (grid_size, grid_size))
    received = moved[0].reshape(orbitals.shape[1:4] + (grid_size, grid_size))
    fft_count = lax.axis_size("fft")
    fft_rank = lax.axis_index("fft")
    pool_count = lax.axis_size("pool")
    pool_rank = lax.axis_index("pool")
    shift_q = momentum(kpoint_grid, pool_rank, pool_count)
    forward = dft_table(grid_size, -1.0)
    backward = dft_table(grid_size, 1.0)
    column_share = grid_size * grid_size // fft_count
    share_ids = fft_rank * column_share + jnp.arange(column_share, dtype=jnp.int32)
    ordered_map = jnp.sort(stick_map)
    found_at = jnp.searchsorted(ordered_map, share_ids)
    found_at = jnp.minimum(found_at, stick_map.shape[0] - 1)
    own_present = jnp.take(ordered_map, found_at) == share_ids
    weights = kernel_table(jnp.where(own_present, share_ids, -1), shift_q, grid_size)

    def potential(pair_block):
        along_x = apply_table(pair_block, forward, "pczyx,cxek->pezyk").astype(jnp.bfloat16)
        along_y = apply_table(along_x, forward, "pczyx,cyek->pezkx").astype(jnp.bfloat16)
        piece_block = lax.all_to_all(along_y, "fft", split_axis=3, concat_axis=2, tiled=True)
        flat_piece = piece_block.reshape(piece_block.shape[:3] + (column_share,))
        scaled_back = column_pass(flat_piece, weights, forward, backward).reshape(piece_block.shape)
        spectrum = lax.all_to_all(scaled_back, "fft", split_axis=2, concat_axis=3, tiled=True)
        back_y = apply_table(spectrum, backward, "pczkx,ckey->pezyx").astype(jnp.bfloat16)
        return apply_table(back_y, backward, "pczyk,ckex->pezyx")

    density = pair_density(own_bands, received)
    field = lax.map(lambda single_pair: potential(single_pair[None])[0], density)
    result = action_of(received, field)
    return result.reshape((1,) + result.shape[:3] + (grid_size * grid_size,))


def solution(mesh):
    return jax.shard_map(
        local,
        mesh=mesh,
        in_specs=(P("pool", None, None, "fft", None), P(), P()),
        out_specs=P("pool", None, None, "fft", None),
        check_vma=False,
    )
```

profile of v0, /device:TPU:0, one launch (start us, length us, event | category | flops | bytes accessed | tf_op | source)
XLA Modules:
  0.0 470.6 jit_solution(1656870052998849744)
XLA Ops:
  0.0 3.1 collective-permute-start
  3.1 8.6 %sort.15 = (s32[16000]{0:T(1024)S(1)}, s32[16000]{0:T(1024)}) sort(s32[16000]{0:T(1024)} %param.6, s32[16000]{0:T(1024)S(1)} %iota.64), dimensions={0}, to_apply=%region_0.1 | sort | flops 224000 | bytes 256000 | tf_op jit(solution)/shard_map/jit(sort)/sort | solution.py:114
  11.7 238.8 %while.28 = (s32[]{:T(128)}, u32[3200]{0:T(1024)S(1)}, u32[3200]{0:T(1024)S(1)}, s32[16000]{0:T(1024)S(1)}, s32[]{:T(128)}, /*index=5*/s32[]{:T(128)}, s32[]{:T(128)}, s32[]{}) while((s32[]{:T(128)}, u32[3200]{0:T(1024)S(1)}, u32[3200]{0:T(1024)S(1)}, s32[16000]{0:T(1024)S(1)}, s32[]{:T(128)}, /*index=5*/s32[]{:T(128)}, s32[]{:T(128)}, ...), condition=%wide.region_2.3_spmd.clone, body=%wide.region_1.2_spmd.clone.sunk | while | flops 64900 | bytes 227697 | solution.py:115
  11.9 16.9 %gather_fusion = s32[3200]{0:T(1024)S(1)} fusion(s32[16000]{0:T(1024)S(1)} %get-tuple-element.202, u32[4096]{0:T(1024)S(1)} %pad_clamp_fusion.3), kind=kCustom, calls=%fused_computation.clone.clone.1 | custom fusion | bytes 38400 | tf_op jit(solution)/shard_map/jit(searchsorted)/jit(_searchsorted_scan_impl)/vmap(jit(_searchsorted_scan_impl))/while/body/eval_jaxpr/gather | solution.py:115
  28.9 16.9 %gather_fusion = s32[3200]{0:T(1024)S(1)} fusion(s32[16000]{0:T(1024)S(1)} %get-tuple-element.202, u32[4096]{0:T(1024)S(1)} %pad_clamp_fusion.3), kind=kCustom, calls=%fused_computation.clone.clone.1 | custom fusion | bytes 38400 | tf_op jit(solution)/shard_map/jit(searchsorted)/jit(_searchsorted_scan_impl)/vmap(jit(_searchsorted_scan_impl))/while/body/eval_jaxpr/gather | solution.py:115
  46.0 16.9 %gather_fusion = s32[3200]{0:T(1024)S(1)} fusion(s32[16000]{0:T(1024)S(1)} %get-tuple-element.202, u32[4096]{0:T(1024)S(1)} %pad_clamp_fusion.3), kind=kCustom, calls=%fused_computation.clone.clone.1 | custom fusion | bytes 38400 | tf_op jit(solution)/shard_map/jit(searchsorted)/jit(_searchsorted_scan_impl)/vmap(jit(_searchsorted_scan_impl))/while/body/eval_jaxpr/gather | solution.py:115
  63.0 16.9 %gather_fusion = s32[3200]{0:T(1024)S(1)} fusion(s32[16000]{0:T(1024)S(1)} %get-tuple-element.202, u32[4096]{0:T(1024)S(1)} %pad_clamp_fusion.3), kind=kCustom, calls=%fused_computation.clone.clone.1 | custom fusion | bytes 38400 | tf_op jit(solution)/shard_map/jit(searchsorted)/jit(_searchsorted_scan_impl)/vmap(jit(_searchsorted_scan_impl))/while/body/eval_jaxpr/gather | solution.py:115
  80.0 16.9 %gather_fusion = s32[3200]{0:T(1024)S(1)} fusion(s32[16000]{0:T(1024)S(1)} %get-tuple-element.202, u32[4096]{0:T(1024)S(1)} %pad_clamp_fusion.3), kind=kCustom, calls=%fused_computation.clone.clone.1 | custom fusion | bytes 38400 | tf_op jit(solution)/shard_map/jit(searchsorted)/jit(_searchsorted_scan_impl)/vmap(jit(_searchsorted_scan_impl))/while/body/eval_jaxpr/gather | solution.py:115
  97.1 16.9 %gather_fusion = s32[3200]{0:T(1024)S(1)} fusion(s32[16000]{0:T(1024)S(1)} %get-tuple-element.202, u32[4096]{0:T(1024)S(1)} %pad_clamp_fusion.3), kind=kCustom, calls=%fused_computation.clone.clone.1 | custom fusion | bytes 38400 | tf_op jit(solution)/shard_map/jit(searchsorted)/jit(_searchsorted_scan_impl)/vmap(jit(_searchsorted_scan_impl))/while/body/eval_jaxpr/gather | solution.py:115
  114.1 16.9 %gather_fusion = s32[3200]{0:T(1024)S(1)} fusion(s32[16000]{0:T(1024)S(1)} %get-tuple-element.202, u32[4096]{0:T(1024)S(1)} %pad_clamp_fusion.3), kind=kCustom, calls=%fused_computation.clone.clone.1 | custom fusion | bytes 38400 | tf_op jit(solution)/shard_map/jit(searchsorted)/jit(_searchsorted_scan_impl)/vmap(jit(_searchsorted_scan_impl))/while/body/eval_jaxpr/gather | solution.py:115
  131.2 16.9 %gather_fusion = s32[3200]{0:T(1024)S(1)} fusion(s32[16000]{0:T(1024)S(1)} %get-tuple-element.202, u32[4096]{0:T(1024)S(1)} %pad_clamp_fusion.3), kind=kCustom, calls=%fused_computation.clone.clone.1 | custom fusion | bytes 38400 | tf_op jit(solution)/shard_map/jit(searchsorted)/jit(_searchsorted_scan_impl)/vmap(jit(_searchsorted_scan_impl))/while/body/eval_jaxpr/gather | solution.py:115
  148.2 16.9 %gather_fusion = s32[3200]{0:T(1024)S(1)} fusion(s32[16000]{0:T(1024)S(1)} %get-tuple-element.202, u32[4096]{0:T(1024)S(1)} %pad_clamp_fusion.3), kind=kCustom, calls=%fused_computation.clone.clone.1 | custom fusion | bytes 38400 | tf_op jit(solution)/shard_map/jit(searchsorted)/jit(_searchsorted_scan_impl)/vmap(jit(_searchsorted_scan_impl))/while/body/eval_jaxpr/gather | solution.py:115
  165.3 16.9 %gather_fusion = s32[3200]{0:T(1024)S(1)} fusion(s32[16000]{0:T(1024)S(1)} %get-tuple-element.202, u32[4096]{0:T(1024)S(1)} %pad_clamp_fusion.3), kind=kCustom, calls=%fused_computation.clone.clone.1 | custom fusion | bytes 38400 | tf_op jit(solution)/shard_map/jit(searchsorted)/jit(_searchsorted_scan_impl)/vmap(jit(_searchsorted_scan_impl))/while/body/eval_jaxpr/gather | solution.py:115
  182.3 16.9 %gather_fusion = s32[3200]{0:T(1024)S(1)} fusion(s32[16000]{0:T(1024)S(1)} %get-tuple-element.202, u32[4096]{0:T(1024)S(1)} %pad_clamp_fusion.3), kind=kCustom, calls=%fused_computation.clone.clone.1 | custom fusion | bytes 38400 | tf_op jit(solution)/shard_map/jit(searchsorted)/jit(_searchsorted_scan_impl)/vmap(jit(_searchsorted_scan_impl))/while/body/eval_jaxpr/gather | solution.py:115
  199.4 16.9 %gather_fusion = s32[3200]{0:T(1024)S(1)} fusion(s32[16000]{0:T(1024)S(1)} %get-tuple-element.202, u32[4096]{0:T(1024)S(1)} %pad_clamp_fusion.3), kind=kCustom, calls=%fused_computation.clone.clone.1 | custom fusion | bytes 38400 | tf_op jit(solution)/shard_map/jit(searchsorted)/jit(_searchsorted_scan_impl)/vmap(jit(_searchsorted_scan_impl))/while/body/eval_jaxpr/gather | solution.py:115
  216.4 16.9 %gather_fusion = s32[3200]{0:T(1024)S(1)} fusion(s32[16000]{0:T(1024)S(1)} %get-tuple-element.202, u32[4096]{0:T(1024)S(1)} %pad_clamp_fusion.3), kind=kCustom, calls=%fused_computation.clone.clone.1 | custom fusion | bytes 38400 | tf_op jit(solution)/shard_map/jit(searchsorted)/jit(_searchsorted_scan_impl)/vmap(jit(_searchsorted_scan_impl))/while/body/eval_jaxpr/gather | solution.py:115
  233.4 16.9 %gather_fusion = s32[3200]{0:T(1024)S(1)} fusion(s32[16000]{0:T(1024)S(1)} %get-tuple-element.202, u32[4096]{0:T(1024)S(1)} %pad_clamp_fusion.3), kind=kCustom, calls=%fused_computation.clone.clone.1 | custom fusion | bytes 38400 | tf_op jit(solution)/shard_map/jit(searchsorted)/jit(_searchsorted_scan_impl)/vmap(jit(_searchsorted_scan_impl))/while/body/eval_jaxpr/gather | solution.py:115
  251.9 0.7 cosine_convert_fusion
  252.6 0.7 negate_convert_fusion.2
  253.3 0.8 fusion.54
  254.1 19.3 %fusion.44 = (bf16[20,25600]{1,0:T(8,128)(2,1)}, bf16[20,25600]{1,0:T(8,128)(2,1)S(1)}) fusion(bf16[1,2,1,20,25600]{4,1,3,2,0:T(2,128)(2,1)} %param.5, bf16[1,2,1,20,25600]{4,1,3,2,0:T(2,128)(2,1)S(1)} %collective-permute-done), kind=kLoop, calls=%fused_computation.59 | loop fusion | flops 6144000 | bytes 6144000 | tf_op jit(solution)/shard_map/convert.5
  273.4 4.3 add.213
  277.7 3.1 sub.60
  280.9 7.6 %fusion.10 = bf16[1,2,20,160,160]{4,3,2,1,0:T(8,128)(2,1)} fusion(bf16[1,1,1,20,160,160]{5,4,2,3,1,0:T(8,128)(2,1)} %bitcast.197, bf16[1,1,1,20,160,160]{5,4,2,3,1,0:T(8,128)(2,1)} %bitcast.196, bf16[1,160,2,160]{1,3,0,2:T(8,128)(2,1)} %get-tuple-element.136, bf16[1,160,2,160]{1,3,0,2:T(8,128)(2,1)} %get-tuple-element.137), kind=kOutput, calls=%fused_computation.21 | convolution fusion | flops 1317683200 | bytes 4300800 | tf_op jit(solution)/shard_map/while/body/eval_jaxpr/pczyx,cyek->pezkx/dot_general | solution.py:91
  288.5 7.0 %copy.57 = bf16[1,2,20,160,160]{4,1,2,0,3:T(2,128)(2,1)} copy(bf16[1,2,20,160,160]{4,3,2,1,0:T(8,128)(2,1)} %fusion.10) | data formatting | bytes 4096000 | tf_op jit(solution)/shard_map/while/body/eval_jaxpr/convert_element_type | solution.py:122
  295.4 4.7 %all-to-all-start = ((bf16[1,2,20,160,160]{4,1,2,0,3:T(2,128)(2,1)}), bf16[1,2,20,160,160]{4,1,2,0,3:T(2,128)(2,1)}, u32[]{:S(2)}, u32[]{:S(2)}) async-start(bf16[1,2,20,160,160]{4,1,2,0,3:T(2,128)(2,1)} %copy.57), calls=%async_computation | async-start | bytes 6553600 | tf_op jit(solution)/shard_map/while/body/eval_jaxpr/all_to_all | solution.py:123
  300.2 16.9 %gather_fusion.1 = s32[3200]{0:T(1024)S(1)} fusion(s32[16000]{0:T(1024)S(1)} %get-tuple-element.207, s32[4096]{0:T(1024)S(1)} %pad_clamp_fusion.1), kind=kCustom, calls=%fused_computation.1 | custom fusion | bytes 38400 | tf_op jit(solution)/shard_map/jit(_take)/gather | solution.py:117
  317.8 1.2 multiply_add_fusion
  319.0 2.8 fusion.32
  321.8 17.6 %all-to-all-done = bf16[1,2,20,160,160]{4,1,2,0,3:T(2,128)(2,1)} async-done(((bf16[1,2,20,160,160]{4,1,2,0,3:T(2,128)(2,1)}), bf16[1,2,20,160,160]{4,1,2,0,3:T(2,128)(2,1)}, u32[]{:S(2)}, u32[]{:S(2)}) %all-to-all-start) | async-done | bytes 2048032 | tf_op jit(solution)/shard_map/while/body/eval_jaxpr/all_to_all | solution.py:123
  339.4 5.1 %copy.58 = bf16[1,2,20,160,160]{4,1,3,2,0:T(2,128)(2,1)S(1)} copy(bf16[1,2,20,160,160]{4,1,2,0,3:T(2,128)(2,1)} %all-to-all-done) | data formatting | bytes 4096000 | tf_op jit(solution)/shard_map/while/body/eval_jaxpr/all_to_all | solution.py:123
  344.6 2.6 copy.59
  347.1 6.6 %reshape.578 = bf16[2,160,3200,1]{2,1,0,3:T(8,128)(2,1)} reshape(bf16[1,2,8,20,20,160]{5,4,3,2,1,0:T(8,128)(2,1)} %copy.59) | data formatting | bytes 4096000 | tf_op jit(solution)/shard_map/reshape.20
  353.7 5.9 %fusion.4 = bf16[2,160,3200]{2,1,0:T(8,128)(2,1)} fusion(bf16[2,160,3200,1]{2,1,0,3:T(8,128)(2,1)} %reshape.578, f32[160,3200]{1,0:T(8,128)} %fusion.32, bf16[1,160,2,160]{1,3,0,2:T(8,128)(2,1)S(1)} %copy-done.1, bf16[1,160,2,160]{1,3,0,2:T(8,128)(2,1)S(1)} %copy-done.2, bf16[1,160,2,160]{1,3,2,0:T(8,128)(2,1)S(1)} %copy-done, ...), kind=kOutput, calls=%fused_computation.15 | convolution fusion | flops 1313996800 | bytes 6553600 | tf_op jit(solution)/shard_map/while/body/eval_jaxpr/pczs,czdk->pdks/dot_general | solution.py:91
  359.6 7.5 %reshape.548 = bf16[1,2,160,20,160]{4,3,2,1,0:T(8,128)(2,1)} reshape(bf16[2,160,3200]{2,1,0:T(8,128)(2,1)} %fusion.4) | data formatting | bytes 4096000 | tf_op jit(solution)/shard_map/while/body/eval_jaxpr/reshape | solution.py:125
  367.2 7.2 %copy.60 = bf16[1,2,160,20,160]{4,1,3,0,2:T(2,128)(2,1)S(1)} copy(bf16[1,2,160,20,160]{4,3,2,1,0:T(8,128)(2,1)} %reshape.548) | data formatting | bytes 4096000 | tf_op jit(solution)/shard_map/while/body/eval_jaxpr/reshape | solution.py:125
  374.3 41.8 %all_to_all.38 = bf16[1,2,160,20,160]{4,1,3,0,2:T(2,128)(2,1)S(1)} all-to-all(bf16[1,2,160,20,160]{4,1,3,0,2:T(2,128)(2,1)S(1)} %copy.60), channel_id=1, replica_groups=mesh['pool'=4,'fft'=8] {'fft'}, dimensions={2} | all-to-all | bytes 4096000 | tf_op jit(solution)/shard_map/while/body/eval_jaxpr/all_to_all | solution.py:126
  416.2 3.2 copy.61
  419.4 1.9 fusion.9
  421.3 1.9 fusion.20
  423.2 3.1 fusion.71
  426.3 5.2 %copy.67 = f32[1,1,1,20,160,160]{5,4,2,3,1,0:T(8,128)} copy(f32[1,1,1,20,160,160]{4,5,3,2,1,0:T(8,128)} %get-tuple-element.131) | data formatting | bytes 4096000 | tf_op jit(solution)/shard_map/slice | solution.py:84
  431.5 5.9 %squeeze.35 = f32[1,1,1,20,25600]{4,2,3,1,0:T(1,128)} reshape(f32[1,1,1,20,160,160]{5,4,2,3,1,0:T(8,128)} %copy.67) | data formatting | bytes 4096000 | tf_op jit(solution)/shard_map/squeeze | solution.py:84
  437.4 5.2 %copy.66 = f32[1,1,1,20,160,160]{5,4,2,3,1,0:T(8,128)} copy(f32[1,1,1,20,160,160]{4,5,3,2,1,0:T(8,128)} %get-tuple-element.132) | data formatting | bytes 4096000 | tf_op jit(solution)/shard_map/slice | solution.py:83
  442.6 5.9 %squeeze.34 = f32[1,1,1,20,25600]{4,2,3,1,0:T(1,128)} reshape(f32[1,1,1,20,160,160]{5,4,2,3,1,0:T(8,128)} %copy.66) | data formatting | bytes 4096000 | tf_op jit(solution)/shard_map/squeeze | solution.py:83
  448.5 9.1 %negate_convert_fusion.1 = (bf16[1,1,1,20,25600]{4,2,3,1,0:T(2,128)(2,1)S(1)}, bf16[1,1,1,20,25600]{4,2,3,1,0:T(2,128)(2,1)}) fusion(f32[1,1,1,20,25600]{4,2,3,1,0:T(1,128)} %squeeze.35, f32[1,1,1,20,25600]{4,2,3,1,0:T(1,128)} %squeeze.34, bf16[1,2,1,20,25600]{4,1,3,2,0:T(2,128)(2,1)S(1)} %collective-permute-done), kind=kLoop, calls=%fused_computation.56 | loop fusion | flops 6144000 | bytes 8192000 | tf_op jit(solution)/shard_map/convert
  457.6 8.3 %pad_maximum_fusion = bf16[1,2,1,20,25600]{4,2,3,1,0:T(2,128)(2,1)S(1)} fusion(bf16[1,1,1,20,25600]{4,2,3,1,0:T(2,128)(2,1)} %get-tuple-element.134, bf16[1,1,1,20,25600]{4,2,3,1,0:T(2,128)(2,1)S(1)} %get-tuple-element.133), kind=kLoop, calls=%fused_computation.17 | loop fusion | flops 1024000 | bytes 4096000 | tf_op jit(solution)/shard_map/stack | solution.py:87
  465.9 4.5 copy.68
  (93 shorter events, 2.7 us)
Async XLA Ops:
  0.0 254.1 %collective-permute-start = (bf16[1,2,1,20,25600]{4,1,3,2,0:T(2,128)(2,1)}, bf16[1,2,1,20,25600]{4,1,3,2,0:T(2,128)(2,1)S(1)}, u32[]{:S(2)}, u32[]{:S(2)}) collective-permute-start(bf16[1,2,1,20,25600]{4,1,3,2,0:T(2,128)(2,1)} %param.5), channel_id=1, source_target_pairs={{0,8},{8,16},{16,24},{24,0},{1,9},{9,17},{17,25},{25,1},{2,10},{10... | collective-permute-start | bytes 6144008 | tf_op jit(solution)/shard_map/ppermute | solution.py:19
  11.7 238.8 %copy-start.3 = (s32[4,3]{1,0:T(4,128)S(1)}, s32[4,3]{1,0:T(4,128)}, u32[]{:S(2)}) copy-start(s32[4,3]{1,0:T(4,128)} %param.7) | copy-start | bytes 148
  295.4 44.0 %all-to-all-start = ((bf16[1,2,20,160,160]{4,1,2,0,3:T(2,128)(2,1)}), bf16[1,2,20,160,160]{4,1,2,0,3:T(2,128)(2,1)}, u32[]{:S(2)}, u32[]{:S(2)}) async-start(bf16[1,2,20,160,160]{4,1,2,0,3:T(2,128)(2,1)} %copy.57), calls=%async_computation | async-start | bytes 6553600 | tf_op jit(solution)/shard_map/while/body/eval_jaxpr/all_to_all | solution.py:123
  347.1 6.6 %copy-start = (bf16[1,160,2,160]{1,3,2,0:T(8,128)(2,1)S(1)}, bf16[1,160,2,160]{1,3,2,0:T(8,128)(2,1)}, u32[]{:S(2)}) copy-start(bf16[1,160,2,160]{1,3,2,0:T(8,128)(2,1)} %get-tuple-element.138) | copy-start | bytes 307204
  347.1 6.6 %copy-start.1 = (bf16[1,160,2,160]{1,3,0,2:T(8,128)(2,1)S(1)}, bf16[1,160,2,160]{1,3,0,2:T(8,128)(2,1)}, u32[]{:S(2)}) copy-start(bf16[1,160,2,160]{1,3,0,2:T(8,128)(2,1)} %get-tuple-element.136) | copy-start | bytes 307204
  347.1 6.6 %copy-start.2 = (bf16[1,160,2,160]{1,3,0,2:T(8,128)(2,1)S(1)}, bf16[1,160,2,160]{1,3,0,2:T(8,128)(2,1)}, u32[]{:S(2)}) copy-start(bf16[1,160,2,160]{1,3,0,2:T(8,128)(2,1)} %get-tuple-element.137) | copy-start | bytes 307204
where the time goes:
time: 476 us; the launch traced here: 471 us
  local copies, waits for them, and re-layouts  331 us (70%)
  other arithmetic  53.5 us (11%)
  blocking collectives  41.8 us (9%)
  waiting for transfers between devices  17.6 us (4%)
  matrix products  17.3 us (4%)
  starting transfers between devices  7.76 us (2%)
    gather x14, local copies, waits for them, and re-layouts, local(): found_at = jnp.searchsorted(ordered_map, share_ids)  237 us
    all_to_all x1, blocking collectives, potential(): lax.all_to_all(scaled_back, 'fft', split_axis=2, concat_axis=3, tiled=True)  41.8 us
    another operation x5, other arithmetic  30.4 us
    all_to_all x1, waiting for transfers between devices, potential(): lax.all_to_all(along_y, 'fft', split_axis=3, concat_axis=2, tiled=True)  17.6 us
    dot_general x4, matrix products, apply_table(): return jnp.einsum(form, data, table, preferred_element_type=jnp.float32)  17.3 us
    gather x1, local copies, waits for them, and re-layouts, local(): own_present = jnp.take(ordered_map, found_at) == share_ids  16.9 us
    reshape x2, local copies, waits for them, and re-layouts, potential(): column_pass(flat_piece, weights, forward, backward)  14.7 us
  transfers between devices with their start and end apart: 2, of which 1 were waited for; matrix products, arithmetic and copies ran while one was open for 58% of the time, Pallas kernels for 0%

commit v1 on v0

v1 whole, which is shorter than its diff:
```python
import functools
import math

import jax
import jax.numpy as jnp
import numpy as np
from jax import lax
from jax.experimental import pallas as pl
from jax.experimental.pallas import tpu as pltpu
from jax.sharding import PartitionSpec as P

KMESH = 4
SPACING_BOHR = 0.1875
SCREENING = 0.106
LANES = 128
BF = jnp.bfloat16
F32 = jnp.float32


def up(value, unit):
    return -(-value // unit) * unit


def lane_order(grid):
    half = LANES // 2
    low = np.concatenate([np.arange(half), np.arange(grid - half, grid)])
    high = np.arange(half, grid - half)
    assert high.size <= half
    return low, high


def trig(grid):
    n = np.arange(grid)
    angle = ((n[:, None] * n[None, :]) % grid).astype(np.float32) * np.float32(2.0 * math.pi / grid)
    return np.cos(angle), np.sin(angle)


def x_forward(grid, group):
    low, high = lane_order(grid)
    c, s = trig(grid)
    margin = LANES - math.gcd(grid, LANES)
    table = np.zeros((2, margin + 2 * LANES, 3 * LANES), np.float32)
    rows = slice(margin, margin + grid)
    for part in range(2):
        re = c if part == 0 else s
        im = -s if part == 0 else c
        table[part, rows, :LANES] = re[:, low]
        table[part, rows, LANES : 2 * LANES] = im[:, low]
        table[part, rows, 2 * LANES : 2 * LANES + high.size] = re[:, high]
        table[part, rows, 2 * LANES + LANES // 2 : 2 * LANES + LANES // 2 + high.size] = im[:, high]
    return table, margin


def x_backward(grid, group):
    low, high = lane_order(grid)
    c, s = trig(grid)
    table = np.zeros((group, 3 * LANES, 4 * LANES), np.float32)
    for j in range(group):
        off = grid * j % LANES
        re, im = slice(off, off + grid), slice(2 * LANES + off, 2 * LANES + off + grid)
        second = 2 * LANES + LANES // 2
        table[j, :LANES, re], table[j, :LANES, im] = c[low], s[low]
        table[j, LANES : 2 * LANES, re], table[j, LANES : 2 * LANES, im] = -s[low], c[low]
        table[j, 2 * LANES : 2 * LANES + high.size, re] = c[high]
        table[j, 2 * LANES : 2 * LANES + high.size, im] = s[high]
        table[j, second : second + high.size, re] = -s[high]
        table[j, second : second + high.size, im] = c[high]
    return table


def left(grid, sign, outer, inner, padded, order=None):
    c, s = trig(grid)
    table = np.zeros((grid, 2, outer, padded), np.float32)
    table[:, 0, :, :inner] = c.T.reshape(grid, outer, inner)
    table[:, 1, :, :inner] = sign * s.T.reshape(grid, outer, inner)
    table = table.reshape(grid, 2 * outer * padded)
    return table if order is None else table[order]


def turned(re, im, mix):
    lane = lax.broadcasted_iota(jnp.int32, mix.shape, 1)
    rolled = pltpu.roll(mix, LANES // 2, 1)
    swapped = jnp.where(lane < LANES // 2, -rolled, rolled)
    top = jnp.concatenate([re, im, mix], axis=1).astype(BF)
    bottom = jnp.concatenate([-im, re, swapped], axis=1).astype(BF)
    return jnp.concatenate([top, bottom], axis=0)


def dot(a, b):
    return jnp.dot(a, b, preferred_element_type=F32)


def tile(value, t):
    return value[:, t * LANES : (t + 1) * LANES]


def forward_kernel(grid, group, margin, own, rec, wx, fy, out, dens, xs, ys):
    planes = own.shape[2]
    span = grid * group
    count = grid // group
    depth = dens.shape[2]
    tall = up(planes, 8)
    chunk = planes * planes

    def pair(g, _):
        lanes = pl.ds(pl.multiple_of(g * span, LANES), span)
        ur, ui = own[0, 0, :, lanes].astype(F32), own[1, 0, :, lanes].astype(F32)
        rr, ri = rec[0, 0, :, lanes].astype(F32), rec[1, 0, :, lanes].astype(F32)
        dens[0, g, :planes, :] = (rr * ur + ri * ui).astype(BF)
        dens[1, g, :planes, :] = (rr * ui - ri * ur).astype(BF)
        return 0

    lax.fori_loop(0, count, pair, 0)
    step = 8
    for j in range(group):
        start = grid * j // LANES * LANES
        shift = margin - grid * j % LANES
        weight = jnp.concatenate([wx[0, shift : shift + 2 * LANES], wx[1, shift : shift + 2 * LANES]], axis=0)

        def along_x(b, _):
            g0 = b * step
            parts = [dens[p, pl.ds(g0, step), :, start : start + 2 * LANES].reshape(step * depth, 2 * LANES) for p in range(2)]
            got = dot(jnp.concatenate(parts, axis=1), weight)
            for i in range(step):
                for t in range(3):
                    xs[t, pl.ds((g0 + i) * group + j, tall, stride=grid), :] = tile(got[i * depth : i * depth + tall], t)
            return 0

        lax.fori_loop(0, count // step, along_x, 0)

    def along_y(z, _):
        rows = pl.ds(pl.multiple_of(z * grid, 8), grid)
        got = dot(fy[...], turned(xs[0, rows, :], xs[1, rows, :], xs[2, rows, :]))
        for t in range(3):
            ys[t, pl.ds(z, grid, stride=planes), :] = tile(got, t)
        return 0

    lax.fori_loop(0, planes, along_y, 0)
    for d in range(out.shape[0]):
        for t in range(3):
            out[d, t] = ys[t, d * chunk : (d + 1) * chunk, :].astype(BF)


def gathered(held, t, first, planes):
    tall = up(planes, 8)
    return jnp.concatenate([held[s, t, pl.ds(first, tall), :] for s in range(held.shape[0])], axis=0)


def widen(source, held):
    rows = source.shape[2]
    for s in range(source.shape[0]):
        for t in range(3):
            held[s, t, :rows, :] = source[s, t].astype(F32)
            held[s, t, rows:, :] = jnp.zeros((held.shape[2] - rows, LANES), F32)


def column_kernel(grid, planes, source, weights, fz, bz, out, held, cs):
    chunk = planes * planes
    widen(source, held)

    def column(k, _):
        first = k * planes
        got = dot(fz[...], turned(*[gathered(held, t, first, planes) for t in range(3)]))
        low, high = weights[k, :, :LANES], weights[k, :, LANES:]
        scaled = [tile(got, 0) * low, tile(got, 1) * low, tile(got, 2) * high]
        back = dot(bz[...], turned(*scaled))
        for t in range(3):
            cs[t, pl.ds(k, grid, stride=planes), :] = tile(back, t)
        return 0

    lax.fori_loop(0, planes, column, 0)
    for s in range(out.shape[0]):
        for t in range(3):
            out[s, t] = cs[t, s * chunk : (s + 1) * chunk, :].astype(BF)


def backward_kernel(grid, group, source, rec, by, wb, out, held, xs):
    planes = rec.shape[2]
    tall = up(planes, 8)
    span = grid * group
    count = grid // group
    widen(source, held)

    def back_y(z, _):
        got = dot(by[...], turned(*[gathered(held, t, z * planes, planes) for t in range(3)]))
        for t in range(3):
            xs[t, pl.ds(z, grid, stride=tall), :] = tile(got, t)
        return 0

    lax.fori_loop(0, planes, back_y, 0)
    step = 4

    def back_x(b, _):
        tiles = {}
        for j in range(group):
            rows = pl.ds(pl.multiple_of((j * count + b * step) * tall, 8), step * tall)
            got = dot(jnp.concatenate([xs[t, rows, :].astype(BF) for t in range(3)], axis=1), wb[j])
            for part in range(2):
                for side in range(2):
                    key = part, grid * j // LANES + side
                    piece = tile(got, 2 * part + side)
                    tiles[key] = piece if key not in tiles else tiles[key] + piece
        field = [jnp.concatenate([tiles[part, t] for t in range(span // LANES)], axis=1) for part in range(2)]
        for i in range(step):
            lanes = pl.ds(pl.multiple_of((b * step + i) * span, LANES), span)
            fr, fi = [f[i * tall : i * tall + planes] for f in field]
            rr, ri = rec[0, 0, :, lanes].astype(F32), rec[1, 0, :, lanes].astype(F32)
            out[0, 0, :, lanes] = (ri * fi - rr * fr).astype(BF)
            out[1, 0, :, lanes] = (-(rr * fi + ri * fr)).astype(BF)
        return 0

    lax.fori_loop(0, count // step, back_x, 0)


def signed(frequency, grid):
    return jnp.where(frequency >= grid // 2, frequency - grid, frequency)


def weight_table(stick_map, kpoint_grid, grid, planes):
    pool_count, pool_rank = lax.axis_size("pool"), lax.axis_index("pool")
    rows = jnp.arange(pool_count, dtype=jnp.int32)
    earlier = (pool_rank + pool_count - 1) % pool_count
    current = jnp.sum(jnp.where((rows == pool_rank)[:, None], kpoint_grid, 0), axis=0)
    previous = jnp.sum(jnp.where((rows == earlier)[:, None], kpoint_grid, 0), axis=0)
    shift = (current - previous).astype(F32) / KMESH
    low, high = lane_order(grid)
    order = np.full((2 * LANES,), -1, np.int32)
    order[:LANES] = low
    order[LANES : LANES + high.size] = high
    order[LANES + LANES // 2 : LANES + LANES // 2 + high.size] = high
    kx = jnp.asarray(order)
    ky = lax.axis_index("fft") * planes + jnp.arange(planes, dtype=jnp.int32)
    live = stick_map >= 0
    slot_y = jnp.where(live, stick_map // grid, -2)
    slot_x = jnp.where(live, stick_map % grid, -2)
    at_y = (ky[:, None] == slot_y[None, :]).astype(BF)
    at_x = (kx[:, None] == slot_x[None, :]).astype(BF)
    present = lax.dot_general(at_y, at_x, (((1,), (1,)), ((), ())), preferred_element_type=F32) > 0.5
    fx, fy = signed(kx, grid), signed(ky, grid)
    fz = signed(jnp.arange(grid, dtype=jnp.int32), grid)
    radius = grid // 2
    flat = fx[None, :] * fx[None, :] + fy[:, None] * fy[:, None]
    inside = (flat[:, None, :] + (fz * fz)[None, :, None] <= radius * radius) & present[:, None, :]
    wx, wy, wz = [f.astype(F32) + q for f, q in ((fx, shift[0]), (fy, shift[1]), (fz, shift[2]))]
    square = (wz * wz)[None, :, None] + ((wx * wx)[None, :] + (wy * wy)[:, None])[:, None, :]
    square = jnp.where(inside, square, 1.0)
    cell = SPACING_BOHR * grid
    exponent = math.pi * math.pi * square / (cell * cell * SCREENING * SCREENING)
    weights = cell * cell / math.pi * -jnp.expm1(-exponent) / square / float(grid) ** 3
    return jnp.where(inside, weights, 0.0)


def call(kernel, shape, scratch, *args):
    whole = pl.BlockSpec(memory_space=pltpu.VMEM)
    return pl.pallas_call(
        kernel,
        out_shape=jax.ShapeDtypeStruct(shape, BF),
        in_specs=[whole] * len(args),
        out_specs=whole,
        scratch_shapes=scratch,
        compiler_params=pltpu.CompilerParams(vmem_limit_bytes=60 * 2**20),
    )(*args)


def local(orbitals, stick_map, kpoint_grid):
    planes, cells = orbitals.shape[3:]
    grid = math.isqrt(cells)
    group = LANES // math.gcd(grid, LANES)
    count = lax.axis_size("fft")
    pool = lax.axis_size("pool")
    tall = up(planes, 8)
    chunk = planes * planes
    const = lambda table: jnp.asarray(table, dtype=BF)

    rec = lax.ppermute(orbitals, "pool", [(p, (p + 1) % pool) for p in range(pool)])
    weights = weight_table(stick_map, kpoint_grid, grid, planes)
    own, rec = orbitals[0], rec[0]
    wx, margin = x_forward(grid, group)
    fy = left(grid, -1.0, 1, grid, grid)
    sent = call(
        functools.partial(forward_kernel, grid, group, margin),
        (count, 3, chunk, LANES),
        [
            pltpu.VMEM((2, grid // group, up(planes, 16), grid * group), BF),
            pltpu.VMEM((3, tall * grid, LANES), F32),
            pltpu.VMEM((3, planes * grid, LANES), F32),
        ],
        own, rec, const(wx), const(fy),
    )
    landed = lax.all_to_all(sent, "fft", split_axis=0, concat_axis=0, tiled=True)
    held = pltpu.VMEM((count, 3, up(chunk, 8) + 8, LANES), F32)
    returned = call(
        functools.partial(column_kernel, grid, planes),
        (count, 3, chunk, LANES),
        [held, pltpu.VMEM((3, planes * grid, LANES), F32)],
        landed, weights,
        const(left(grid, -1.0, count, planes, tall)),
        const(left(grid, 1.0, 1, grid, grid)),
    )
    back = lax.all_to_all(returned, "fft", split_axis=0, concat_axis=0, tiled=True)
    y_order = np.arange(grid).reshape(grid // group, group).T.reshape(-1)
    result = call(
        functools.partial(backward_kernel, grid, group),
        own.shape,
        [held, pltpu.VMEM((3, tall * grid, LANES), F32)],
        back, rec,
        const(left(grid, 1.0, count, planes, tall, y_order)),
        const(x_backward(grid, group)),
    )
    return result[None]


def solution(mesh):
    return jax.shard_map(
        local,
        mesh=mesh,
        in_specs=(P("pool", None, None, "fft", None), P(), P()),
        out_specs=P("pool", None, None, "fft", None),
        check_vma=False,
    )
```

time: 476 us -> 178 us (0.37); the launches traced: 471 us -> 177 us
  local copies, waits for them, and re-layouts: 331 us -> 12.5 us
  Pallas kernels: 0 us -> 50 us
  other arithmetic: 53.5 us -> 6.67 us
  waiting for transfers between devices: 17.6 us -> 63.8 us
  matrix products: 17.3 us -> 2.69 us
  blocking collectives: 41.8 us -> 34.8 us
    gather x15 -> x0, local copies, waits for them, and re-layouts: 254 us -> none  [the longest x14 237 us: local(): found_at = jnp.searchsorted(ordered_map, share_ids)]
    pallas_call x0 -> x3, Pallas kernels: none -> 50 us  [call(): pl.pallas_call(kernel, out_shape=jax.ShapeDtypeStruct(shape, BF), in_spec...]
    ppermute x1, waiting for transfers between devices: 0.01 us -> 42.9 us  [local(): lax.ppermute(orbitals, 'pool', [(p, (p + 1) % pool) for p in range(pool)])]
    another operation x7 -> x0, other arithmetic: 39.6 us -> none
    reshape x2 -> x0, local copies, waits for them, and re-layouts: 14.7 us -> none  [potential(): column_pass(flat_piece, weights, forward, backward)]
    dot_general x4 -> x1, matrix products: 17.3 us -> 2.69 us  [weight_table(): lax.dot_general(at_y, at_x, (((1,), (1,)), ((), ())), preferred_element_t...]
    slice x4 -> x1, local copies, waits for them, and re-layouts: 14.2 us -> 0.65 us  [weight_table(): shift[2]]
    squeeze x2 -> x0, local copies, waits for them, and re-layouts: 11.7 us -> none  [the longest x1 5.86 us: action_of(): real_field = field[:, :, 0]]
  transfers between devices with their start and end apart: 2 -> 2, of which waited for: 1 -> 2; matrix products, arithmetic and copies ran while one was open for 58% -> 8% of each run, Pallas kernels for 0% -> 0%
where the time goes in v1:
time: 178 us; the launch traced here: 177 us
  waiting for transfers between devices  63.8 us (36%)
  Pallas kernels  50 us (28%)
  blocking collectives  34.8 us (20%)
  local copies, waits for them, and re-layouts  12.5 us (7%)
  starting transfers between devices  6.91 us (4%)
  other arithmetic  6.67 us (4%)
  matrix products  2.69 us (2%)
    pallas_call x3, Pallas kernels, call(): pl.pallas_call(kernel, out_shape=jax.ShapeDtypeStruct(shape, BF), in_spec...  50 us
    ppermute x1, waiting for transfers between devices, local(): lax.ppermute(orbitals, 'pool', [(p, (p + 1) % pool) for p in range(pool)])  42.9 us
    all_to_all x1, blocking collectives, local(): lax.all_to_all(returned, 'fft', split_axis=0, concat_axis=0, tiled=True)  34.8 us
    all_to_all x1, waiting for transfers between devices, local(): lax.all_to_all(sent, 'fft', split_axis=0, concat_axis=0, tiled=True)  20.9 us
    broadcast_in_dim x1, local copies, waits for them, and re-layouts, local(): return result[None]  5.1 us
    unnamed x13, local copies, waits for them, and re-layouts  4.95 us
    select_n x1, other arithmetic, weight_table(): return jnp.where(inside, weights, 0.0)  4.11 us
    all_to_all x1, starting transfers between devices, local(): lax.all_to_all(sent, 'fft', split_axis=0, concat_axis=0, tiled=True)  3.86 us
  transfers between devices with their start and end apart: 2, of which 2 were waited for; matrix products, arithmetic and copies ran while one was open for 8% of the time, Pallas kernels for 0%

profile of v1, /device:TPU:0, one launch (start us, length us, event | category | flops | bytes accessed | tf_op | source)
XLA Modules:
  0.0 177.5 jit_solution(13516097293044662970)
XLA Ops:
  0.0 0.0 copy-start.1
  0.0 0.0 copy-start.2
  0.0 3.1 %collective-permute-start = (bf16[1,2,1,20,25600]{4,1,3,2,0:T(2,128)(2,1)}, bf16[1,2,1,20,25600]{4,1,3,2,0:T(2,128)(2,1)S(1)}, u32[]{:S(2)}, u32[]{:S(2)}) collective-permute-start(bf16[1,2,1,20,25600]{4,1,3,2,0:T(2,128)(2,1)} %param.10), channel_id=1, source_target_pairs={{0,8},{8,16},{16,24},{24,0},{1,9},{9,17},{17,25},{25,1},{2,10},{10... | collective-permute-start | bytes 6144008 | tf_op jit(solution)/shard_map/ppermute | solution.py:275
  3.1 3.4 %copy.20 = bf16[1,2,1,20,25600]{4,3,1,2,0:T(8,128)(2,1)} copy(bf16[1,2,1,20,25600]{4,1,3,2,0:T(2,128)(2,1)} %param.10) | data formatting | bytes 4096000 | tf_op args[0]
  6.5 0.0 copy-done.1
  6.5 0.1 fusion.13
  6.6 0.0 copy-done.2
  6.6 0.1 select_reduce_fusion
  6.7 0.3 fusion.25
  6.9 42.9 %collective-permute-done = bf16[1,2,1,20,25600]{4,1,3,2,0:T(2,128)(2,1)S(1)} collective-permute-done((bf16[1,2,1,20,25600]{4,1,3,2,0:T(2,128)(2,1)}, bf16[1,2,1,20,25600]{4,1,3,2,0:T(2,128)(2,1)S(1)}, u32[]{:S(2)}, u32[]{:S(2)}) %collective-permute-start) | collective-permute-done | bytes 2048032 | tf_op jit(solution)/shard_map/ppermute | solution.py:275
  49.9 1.8 %copy.19 = bf16[1,2,1,20,25600]{4,3,1,2,0:T(8,128)(2,1)} copy(bf16[1,2,1,20,25600]{4,1,3,2,0:T(2,128)(2,1)S(1)} %collective-permute-done) | data formatting | bytes 4096000 | tf_op jit(solution)/shard_map/ppermute | solution.py:275
  51.7 20.6 %shard_map.100 = bf16[8,3,400,128]{3,2,1,0:T(8,128)(2,1)} custom-call(bf16[2,1,20,25600]{3,2,1,0:T(8,128)(2,1)} %bitcast.13, bf16[2,1,20,25600]{3,2,1,0:T(8,128)(2,1)} %bitcast.11, bf16[2,352,384]{2,1,0:T(8,128)(2,1)} %constant.96.clone.wx, bf16[160,320]{1,0:T(8,128)(2,1)} %constant.97.clone.fy), custom_call_target="tpu_custom_call" | custom-call | tf_op jit(solution)/shard_map/pallas_call | solution.py:255
  72.3 0.0 copy-start.4
  72.3 0.0 copy-start.3
  72.3 0.0 copy-start.5
  72.3 3.9 %all-to-all-start = ((bf16[8,3,400,128]{3,2,1,0:T(8,128)(2,1)}), bf16[8,3,400,128]{3,2,1,0:T(8,128)(2,1)S(1)}, u32[]{:S(2)}, u32[]{:S(2)}) async-start(bf16[8,3,400,128]{3,2,1,0:T(8,128)(2,1)} %shard_map.100), calls=%async_computation | async-start | bytes 4915200 | tf_op jit(solution)/shard_map/all_to_all | solution.py:290
  76.2 0.7 fusion.18
  76.9 0.7 add_multiply_fusion.2
  77.6 0.7 add_multiply_fusion.1
  78.2 0.0 copy-done.4
  78.2 0.6 add_multiply_fusion
  78.9 0.1 broadcast_add_fusion
  78.9 0.0 copy-done.3
  78.9 0.1 broadcast_add_fusion.1
  79.0 0.0 copy-done.5
  79.0 2.7 %fusion.6 = pred[20,256]{1,0:T(8,128)(4,1)S(1)} fusion(s32[16000]{0:T(1024)S(1)} %get-tuple-element.8, s32[256]{0:T(256)S(1)} %copy-done.5, pred[20,16000]{1,0:T(8,128)(4,1)S(1)} %fusion.25), kind=kOutput, calls=%fused_computation.10 | convolution fusion | flops 167941120 | bytes 390144 | tf_op jit(solution)/shard_map/dot_general | solution.py:238
  81.7 4.1 %multiply_select_fusion.weights = f32[20,160,256]{2,1,0:T(8,128)} fusion(f32[20,256]{1,0:T(8,128)S(1)} %broadcast_add_fusion, f32[160]{0:T(256)S(1)} %add_multiply_fusion.1, s32[160]{0:T(256)S(1)} %fusion.16, s32[20,256]{1,0:T(8,128)S(1)} %broadcast_add_fusion.1, pred[20,256]{1,0:T(8,128)(4,1)S(1)} %fusion.6), kind=kLoop, calls=%fused_computation.4 | loop fusion | flops 9830400 | bytes 3324160 | tf_op jit(solution)/shard_map/jit(_where)/select_n | solution.py:250
  85.8 20.9 %all-to-all-done.source = bf16[8,3,400,128]{3,2,1,0:T(8,128)(2,1)S(1)} async-done(((bf16[8,3,400,128]{3,2,1,0:T(8,128)(2,1)}), bf16[8,3,400,128]{3,2,1,0:T(8,128)(2,1)S(1)}, u32[]{:S(2)}, u32[]{:S(2)}) %all-to-all-start) | async-done | bytes 2457632 | tf_op jit(solution)/shard_map/all_to_all | solution.py:290
  106.7 0.0 copy-start
  106.7 1.5 copy-done
  108.2 14.8 %shard_map.101 = bf16[8,3,400,128]{3,2,1,0:T(8,128)(2,1)} custom-call(bf16[8,3,400,128]{3,2,1,0:T(8,128)(2,1)} %copy-done, f32[20,160,256]{2,1,0:T(8,128)} %multiply_select_fusion.weights, bf16[160,384]{1,0:T(8,128)(2,1)} %constant.98.clone.fz, bf16[160,320]{1,0:T(8,128)(2,1)} %constant.99.clone.bz), custom_call_target="tpu_custom_call" | custom-call | tf_op jit(solution)/shard_map/pallas_call | solution.py:255
  123.0 34.8 %all_to_all.10.source = bf16[8,3,400,128]{3,2,1,0:T(8,128)(2,1)} all-to-all(bf16[8,3,400,128]{3,2,1,0:T(8,128)(2,1)} %shard_map.101), channel_id=1, replica_groups=mesh['pool'=4,'fft'=8] {'fft'}, dimensions={0} | all-to-all | bytes 4915200 | tf_op jit(solution)/shard_map/all_to_all | solution.py:300
  157.8 14.6 %shard_map.102 = bf16[2,1,20,25600]{3,2,1,0:T(8,128)(2,1)} custom-call(bf16[8,3,400,128]{3,2,1,0:T(8,128)(2,1)} %all_to_all.10.source, bf16[2,1,20,25600]{3,2,1,0:T(8,128)(2,1)} %bitcast.12, bf16[160,384]{1,0:T(8,128)(2,1)} %constant.100.clone.by, bf16[4,384,512]{2,1,0:T(8,128)(2,1)} %constant.101.clone.wb), custom_call_target="tpu_custom_call" | custom-call | tf_op jit(solution)/shard_map/pallas_call | solution.py:255
  172.4 5.1 %copy.16 = bf16[1,2,1,20,25600]{4,1,3,2,0:T(2,128)(2,1)} copy(bf16[1,2,1,20,25600]{4,3,1,2,0:T(8,128)(2,1)} %bitcast.14) | data formatting | bytes 4096000 | tf_op jit(solution)/shard_map/broadcast_in_dim | solution.py:310
  (4 shorter events, 0.0 us)
Async XLA Ops:
  0.0 6.5 %copy-start.1 = (s32[16000]{0:T(1024)S(1)}, s32[16000]{0:T(1024)}, u32[]{:S(2)}) copy-start(s32[16000]{0:T(1024)} %param.11) | copy-start | bytes 192004
  0.0 6.6 %copy-start.2 = (s32[4,3]{1,0:T(4,128)S(1)}, s32[4,3]{1,0:T(4,128)}, u32[]{:S(2)}) copy-start(s32[4,3]{1,0:T(4,128)} %param.12) | copy-start | bytes 148
  0.0 49.9 %collective-permute-start = (bf16[1,2,1,20,25600]{4,1,3,2,0:T(2,128)(2,1)}, bf16[1,2,1,20,25600]{4,1,3,2,0:T(2,128)(2,1)S(1)}, u32[]{:S(2)}, u32[]{:S(2)}) collective-permute-start(bf16[1,2,1,20,25600]{4,1,3,2,0:T(2,128)(2,1)} %param.10), channel_id=1, source_target_pairs={{0,8},{8,16},{16,24},{24,0},{1,9},{9,17},{17,25},{25,1},{2,10},{10... | collective-permute-start | bytes 6144008 | tf_op jit(solution)/shard_map/ppermute | solution.py:275
  72.3 5.9 %copy-start.4 = (f32[256]{0:T(256)S(1)}, f32[256]{0:T(256)}, u32[]{:S(2)}) copy-start(f32[256]{0:T(256)} %constant.107) | copy-start | bytes 3076
  72.3 6.6 %copy-start.3 = (s32[256]{0:T(256)S(1)}, s32[256]{0:T(256)}, u32[]{:S(2)}) copy-start(s32[256]{0:T(256)} %constant.106) | copy-start | bytes 3076
  72.3 6.7 %copy-start.5 = (s32[256]{0:T(256)S(1)}, s32[256]{0:T(256)}, u32[]{:S(2)}) copy-start(s32[256]{0:T(256)} %constant.95.clone) | copy-start | bytes 3076
  72.3 34.3 %all-to-all-start = ((bf16[8,3,400,128]{3,2,1,0:T(8,128)(2,1)}), bf16[8,3,400,128]{3,2,1,0:T(8,128)(2,1)S(1)}, u32[]{:S(2)}, u32[]{:S(2)}) async-start(bf16[8,3,400,128]{3,2,1,0:T(8,128)(2,1)} %shard_map.100), calls=%async_computation | async-start | bytes 4915200 | tf_op jit(solution)/shard_map/all_to_all | solution.py:290
  106.7 1.5 copy-start

commit v2 on v1

v2 whole, which is shorter than its diff:
```python
import functools
import math

import jax
import jax.numpy as jnp
import numpy as np
from jax import lax
from jax.experimental import pallas as pl
from jax.experimental.pallas import tpu as pltpu
from jax.sharding import PartitionSpec as P

KMESH = 4
SPACING_BOHR = 0.1875
SCREENING = 0.106
LANES = 128
BF = jnp.bfloat16
F32 = jnp.float32


def up(value, unit):
    return -(-value // unit) * unit


def lane_order(grid):
    half = LANES // 2
    low = np.concatenate([np.arange(half), np.arange(grid - half, grid)])
    high = np.arange(half, grid - half)
    assert high.size <= half
    return low, high


def trig(grid):
    n = np.arange(grid)
    angle = ((n[:, None] * n[None, :]) % grid).astype(np.float32) * np.float32(2.0 * math.pi / grid)
    return np.cos(angle), np.sin(angle)


def x_forward(grid, group):
    low, high = lane_order(grid)
    c, s = trig(grid)
    margin = LANES - math.gcd(grid, LANES)
    table = np.zeros((2, margin + 2 * LANES, 3 * LANES), np.float32)
    rows = slice(margin, margin + grid)
    for part in range(2):
        re = c if part == 0 else s
        im = -s if part == 0 else c
        table[part, rows, :LANES] = re[:, low]
        table[part, rows, LANES : 2 * LANES] = im[:, low]
        table[part, rows, 2 * LANES : 2 * LANES + high.size] = re[:, high]
        table[part, rows, 2 * LANES + LANES // 2 : 2 * LANES + LANES // 2 + high.size] = im[:, high]
    return table, margin


def x_backward(grid, group):
    low, high = lane_order(grid)
    c, s = trig(grid)
    table = np.zeros((group, 3 * LANES, 4 * LANES), np.float32)
    for j in range(group):
        off = grid * j % LANES
        re, im = slice(off, off + grid), slice(2 * LANES + off, 2 * LANES + off + grid)
        second = 2 * LANES + LANES // 2
        table[j, :LANES, re], table[j, :LANES, im] = c[low], s[low]
        table[j, LANES : 2 * LANES, re], table[j, LANES : 2 * LANES, im] = -s[low], c[low]
        table[j, 2 * LANES : 2 * LANES + high.size, re] = c[high]
        table[j, 2 * LANES : 2 * LANES + high.size, im] = s[high]
        table[j, second : second + high.size, re] = -s[high]
        table[j, second : second + high.size, im] = c[high]
    return table


def left(grid, sign, order=None):
    c, s = trig(grid)
    table = np.concatenate([c.T, sign * s.T], axis=1)
    return table if order is None else table[order]


def cuts(planes):
    return [(first, min(8, planes - first)) for first in range(0, planes, 8)]


def left_cut(grid, sign, outer, planes, order=None):
    c, s = trig(grid)
    blocks = []
    for part in (c.T, sign * s.T):
        part = part.reshape(grid, outer, planes)
        for first, size in cuts(planes):
            block = np.zeros((grid, outer, 8), np.float32)
            block[:, :, :size] = part[:, :, first : first + size]
            blocks.append(block.reshape(grid, outer * 8))
    table = np.concatenate(blocks, axis=1)
    return table if order is None else table[order]


def parcel(planes, size):
    rows = planes * size
    seg = up(rows, 16)
    mixed = rows // 2 if planes % 2 == 0 else rows
    return rows, seg, mixed, 2 * seg + up(mixed, 16)


def turned(re, im, mix):
    lane = lax.broadcasted_iota(jnp.int32, mix.shape, 1)
    rolled = pltpu.roll(mix, LANES // 2, 1)
    swapped = jnp.where(lane < LANES // 2, -rolled, rolled)
    top = jnp.concatenate([re, im, mix], axis=1).astype(BF)
    bottom = jnp.concatenate([-im, re, swapped], axis=1).astype(BF)
    return jnp.concatenate([top, bottom], axis=0)


def dot(a, b):
    return jnp.dot(a, b, preferred_element_type=F32)


def tile(value, t):
    return value[:, t * LANES : (t + 1) * LANES]


def pack(source, first, target, planes, size):
    rows, seg, mixed, total = parcel(planes, size)
    target[:rows, :] = source[0, pl.ds(first, rows), :].astype(BF)
    target[seg : seg + rows, :] = source[1, pl.ds(first, rows), :].astype(BF)
    mix = source[2, pl.ds(first, mixed), :]
    if mixed < rows:
        mix = mix + pltpu.roll(source[2, pl.ds(first + mixed, mixed), :], LANES // 4, 1)
    target[2 * seg : 2 * seg + mixed, :] = mix.astype(BF)


def unpack(source, held, planes, size):
    rows, seg, mixed, total = parcel(planes, size)
    held[0, :rows, :] = source[:rows, :].astype(F32)
    held[1, :rows, :] = source[seg : seg + rows, :].astype(F32)
    mix = source[2 * seg : 2 * seg + mixed, :].astype(F32)
    held[2, :mixed, :] = mix
    if mixed < rows:
        held[2, mixed:rows, :] = pltpu.roll(mix, LANES - LANES // 4, 1)
    spare = held.shape[1] - rows
    for t in range(3):
        held[t, rows:, :] = jnp.zeros((spare, LANES), F32)


def gathered(helds, t, place, planes):
    pieces = []
    for (first, size), held in zip(cuts(planes), helds):
        start = place * size if size % 8 else pl.multiple_of(place * size, 8)
        pieces += [held[s, t, pl.ds(start, 8), :] for s in range(held.shape[0])]
    return jnp.concatenate(pieces, axis=0)


def exchange_kernel(grid, group, margin, pools, *refs):
    own, weights, wx, fy, fz, bz, rec, refs = *refs[:7], refs[7:]
    planes = rec.shape[2]
    parts = cuts(planes)
    n = len(parts)
    backs, refs = refs[:n], refs[n:]
    sends, lands, helds, refs = refs[:n], refs[n : 2 * n], refs[2 * n : 3 * n], refs[3 * n :]
    mine, dens, xs, ys, local_sem, pool_send, pool_recv, out_send, out_recv, in_send, in_recv = refs
    devices = backs[0].shape[0]
    span, count = grid * group, grid // group
    me = lax.axis_index("fft")
    pool = lax.axis_index("pool")
    peers = [lax.rem(me + o, devices) for o in range(1, devices)]
    after, before = lax.rem(pool + 1, pools), lax.rem(pool + pools - 1, pools)

    fetch = pltpu.make_async_copy(own, mine, local_sem)
    fetch.start()
    barrier = pltpu.get_barrier_semaphore()
    targets = [{"fft": peer} for peer in peers] + [{"pool": after}, {"pool": before}]
    for target in targets:
        pl.semaphore_signal(barrier, inc=1, device_id=target, device_id_type=pl.DeviceIdType.MESH)
    pl.semaphore_wait(barrier, len(targets))

    moves = []
    for c, (first, size) in enumerate(parts):
        moves.append(
            pltpu.make_async_remote_copy(
                src_ref=own.at[:, :, pl.ds(first, size), :],
                dst_ref=rec.at[:, :, pl.ds(first, size), :],
                send_sem=pool_send.at[c],
                recv_sem=pool_recv.at[c],
                device_id={"pool": after},
                device_id_type=pl.DeviceIdType.MESH,
            )
        )
        moves[c].start()
    fetch.wait()

    def post(c, source, landing, send_sem, recv_sem):
        copies = []
        for o, peer in enumerate(peers):
            copies.append(
                pltpu.make_async_remote_copy(
                    src_ref=source.at[peer],
                    dst_ref=landing.at[me],
                    send_sem=send_sem.at[c, o],
                    recv_sem=recv_sem.at[c, o],
                    device_id={"fft": peer},
                    device_id_type=pl.DeviceIdType.MESH,
                )
            )
            copies[o].start()
        landing[me] = source[me]
        return copies

    outward, inward = [], []
    for c, (first, size) in enumerate(parts):
        moves[c].wait_recv()
        planes_here = slice(first, first + size)

        def pair(g, _):
            lanes = pl.ds(pl.multiple_of(g * span, LANES), span)
            ur, ui = mine[0, 0, planes_here, lanes].astype(F32), mine[1, 0, planes_here, lanes].astype(F32)
            rr, ri = rec[0, 0, planes_here, lanes].astype(F32), rec[1, 0, planes_here, lanes].astype(F32)
            dens[0, g, :size, :] = rr * ur + ri * ui
            dens[1, g, :size, :] = rr * ui - ri * ur
            return 0

        lax.fori_loop(0, count, pair, 0)
        step = count // 2
        for j in range(group):
            start = grid * j // LANES * LANES
            shift = margin - grid * j % LANES
            weight = jnp.concatenate([wx[0, shift : shift + 2 * LANES], wx[1, shift : shift + 2 * LANES]], axis=0)

            def along_x(b, _):
                g0 = b * step
                sides = [dens[p, pl.ds(g0, step), :, start : start + 2 * LANES].reshape(step * 8, 2 * LANES) for p in range(2)]
                got = dot(jnp.concatenate(sides, axis=1).astype(BF), weight)
                for i in range(step):
                    for t in range(3):
                        xs[t, pl.ds((g0 + i) * group + j, 8, stride=grid), :] = tile(got[i * 8 : i * 8 + 8], t)
                return 0

            lax.fori_loop(0, 2, along_x, 0)

        def along_y(z, _):
            rows = pl.ds(pl.multiple_of(z * grid, 8), grid)
            got = dot(fy[...], turned(xs[0, rows, :], xs[1, rows, :], xs[2, rows, :]))
            for t in range(3):
                ys[t, pl.ds(z, grid, stride=size), :] = tile(got, t)
            return 0

        lax.fori_loop(0, size, along_y, 0)
        for d in range(devices):
            pack(ys, d * planes * size, sends[c].at[d], planes, size)
        outward.append(post(c, sends[c], lands[c], out_send, out_recv))

    for c, (first, size) in enumerate(parts):
        for copy in outward[c]:
            copy.wait_recv()
        for s in range(devices):
            unpack(lands[c].at[s], helds[c].at[s], planes, size)
    for c in range(n):
        for copy in outward[c]:
            copy.wait_send()

    for c, (first, size) in enumerate(parts):

        def column(k, _):
            place = first + k
            got = dot(fz[...], turned(*[gathered(helds, t, place, planes) for t in range(3)]))
            low, high = weights[place, :, :LANES], weights[place, :, LANES:]
            scaled = [tile(got, 0) * low, tile(got, 1) * low, tile(got, 2) * high]
            back = dot(bz[...], turned(*scaled))
            for t in range(3):
                ys[t, pl.ds(k, grid, stride=size), :] = tile(back, t)
            return 0

        lax.fori_loop(0, size, column, 0)
        for d in range(devices):
            pack(ys, d * planes * size, sends[c].at[d], planes, size)
        inward.append(post(c, sends[c], backs[c], in_send, in_recv))

    for c in range(n):
        for copy in inward[c]:
            copy.wait_recv()
            copy.wait_send()
        moves[c].wait_send()


def backward_kernel(grid, group, *refs):
    planes = refs[0].shape[2]
    parts = cuts(planes)
    n = len(parts)
    rec, by, wb, sources, out = refs[0], refs[1], refs[2], refs[3 : 3 + n], refs[3 + n]
    helds, xs = refs[4 + n : 4 + 2 * n], refs[4 + 2 * n]
    tall = up(planes, 8)
    span = grid * group
    count = grid // group

    @pl.when(pl.program_id(0) == 0)
    def _():
        for c, (first, size) in enumerate(parts):
            for s in range(sources[c].shape[0]):
                unpack(sources[c].at[s], helds[c].at[s], planes, size)

        def back_y(z, _):
            got = dot(by[...], turned(*[gathered(helds, t, z, planes) for t in range(3)]))
            for t in range(3):
                xs[t, pl.ds(z, grid, stride=tall), :] = tile(got, t)
            return 0

        lax.fori_loop(0, planes, back_y, 0)

    step = out.shape[3] // span
    tiles = {}
    for j in range(group):
        rows = pl.ds(pl.multiple_of((j * count + pl.program_id(0) * step) * tall, 8), step * tall)
        got = dot(jnp.concatenate([xs[t, rows, :].astype(BF) for t in range(3)], axis=1), wb[j])
        for part in range(2):
            for side in range(2):
                key = part, grid * j // LANES + side
                piece = tile(got, 2 * part + side)
                tiles[key] = piece if key not in tiles else tiles[key] + piece
    field = [jnp.concatenate([tiles[part, t] for t in range(span // LANES)], axis=1) for part in range(2)]
    for i in range(step):
        lanes = slice(i * span, (i + 1) * span)
        fr, fi = [f[i * tall : i * tall + planes] for f in field]
        rr, ri = rec[0, 0, :, lanes].astype(F32), rec[1, 0, :, lanes].astype(F32)
        out[0, 0, :, lanes] = (ri * fi - rr * fr).astype(BF)
        out[1, 0, :, lanes] = (-(rr * fi + ri * fr)).astype(BF)


def signed(frequency, grid):
    return jnp.where(frequency >= grid // 2, frequency - grid, frequency)


def weight_table(stick_map, kpoint_grid, grid, planes):
    pool_count, pool_rank = lax.axis_size("pool"), lax.axis_index("pool")
    rows = jnp.arange(pool_count, dtype=jnp.int32)
    earlier = (pool_rank + pool_count - 1) % pool_count
    current = jnp.sum(jnp.where((rows == pool_rank)[:, None], kpoint_grid, 0), axis=0)
    previous = jnp.sum(jnp.where((rows == earlier)[:, None], kpoint_grid, 0), axis=0)
    shift = (current - previous).astype(F32) / KMESH
    low, high = lane_order(grid)
    order = np.full((2 * LANES,), -1, np.int32)
    order[:LANES] = low
    order[LANES : LANES + high.size] = high
    order[LANES + LANES // 2 : LANES + LANES // 2 + high.size] = high
    kx = jnp.asarray(order)
    ky = lax.axis_index("fft") * planes + jnp.arange(planes, dtype=jnp.int32)
    live = stick_map >= 0
    slot_y = jnp.where(live, stick_map // grid, -2)
    slot_x = jnp.where(live, stick_map % grid, -2)
    at_y = (ky[:, None] == slot_y[None, :]).astype(BF)
    at_x = (kx[:, None] == slot_x[None, :]).astype(BF)
    present = lax.dot_general(at_y, at_x, (((1,), (1,)), ((), ())), preferred_element_type=F32) > 0.5
    fx, fy = signed(kx, grid), signed(ky, grid)
    fz = signed(jnp.arange(grid, dtype=jnp.int32), grid)
    radius = grid // 2
    flat = fx[None, :] * fx[None, :] + fy[:, None] * fy[:, None]
    inside = (flat[:, None, :] + (fz * fz)[None, :, None] <= radius * radius) & present[:, None, :]
    wx, wy, wz = [f.astype(F32) + q for f, q in ((fx, shift[0]), (fy, shift[1]), (fz, shift[2]))]
    square = (wz * wz)[None, :, None] + ((wx * wx)[None, :] + (wy * wy)[:, None])[:, None, :]
    square = jnp.where(inside, square, 1.0)
    cell = SPACING_BOHR * grid
    exponent = math.pi * math.pi * square / (cell * cell * SCREENING * SCREENING)
    weights = cell * cell / math.pi * -jnp.expm1(-exponent) / square / float(grid) ** 3
    return jnp.where(inside, weights, 0.0)


def local(orbitals, stick_map, kpoint_grid):
    planes, cells = orbitals.shape[3:]
    grid = math.isqrt(cells)
    group = LANES // math.gcd(grid, LANES)
    devices = lax.axis_size("fft")
    pools = lax.axis_size("pool")
    const = lambda table: jnp.asarray(table, dtype=BF)
    parts = cuts(planes)
    n = len(parts)
    vmem = pl.BlockSpec(memory_space=pltpu.VMEM)
    parcels = [(devices, parcel(planes, size)[3], LANES) for _, size in parts]
    helds = [pltpu.VMEM((devices, 3, up(planes * size, 8) + 8, LANES), F32) for _, size in parts]
    biggest = max(size for _, size in parts)

    own = orbitals[0]
    weights = weight_table(stick_map, kpoint_grid, grid, planes)
    wx, margin = x_forward(grid, group)
    rec, *backs = pl.pallas_call(
        functools.partial(exchange_kernel, grid, group, margin, pools),
        out_shape=[jax.ShapeDtypeStruct(own.shape, BF)] + [jax.ShapeDtypeStruct(p, BF) for p in parcels],
        in_specs=[pl.BlockSpec(memory_space=pl.ANY)] + [vmem] * 5,
        out_specs=[vmem] * (1 + n),
        scratch_shapes=[pltpu.VMEM(p, BF) for p in parcels]
        + [pltpu.VMEM(p, BF) for p in parcels]
        + helds
        + [
            pltpu.VMEM(own.shape, BF),
            pltpu.VMEM((2, grid // group, 8, grid * group), F32),
            pltpu.VMEM((3, 8 * grid, LANES), F32),
            pltpu.VMEM((3, biggest * grid, LANES), F32),
            pltpu.SemaphoreType.DMA,
            pltpu.SemaphoreType.DMA((n,)),
            pltpu.SemaphoreType.DMA((n,)),
        ]
        + [pltpu.SemaphoreType.DMA((n, devices - 1)) for _ in range(4)],
        compiler_params=pltpu.CompilerParams(vmem_limit_bytes=60 * 2**20, collective_id=0, has_side_effects=True),
    )(own, weights, const(wx), const(left(grid, -1.0)), const(left_cut(grid, -1.0, devices, planes)), const(left(grid, 1.0)))

    y_order = np.arange(grid).reshape(grid // group, group).T.reshape(-1)
    step = 4
    block = pl.BlockSpec(own.shape[:3] + (step * grid * group,), lambda i: (0, 0, 0, i))
    result = pl.pallas_call(
        functools.partial(backward_kernel, grid, group),
        grid=(grid // group // step,),
        out_shape=jax.ShapeDtypeStruct(own.shape, BF),
        in_specs=[block] + [vmem] * (2 + n),
        out_specs=block,
        scratch_shapes=helds + [pltpu.VMEM((3, up(planes, 8) * grid, LANES), F32)],
        compiler_params=pltpu.CompilerParams(vmem_limit_bytes=50 * 2**20),
    )(rec, const(left_cut(grid, 1.0, devices, planes, y_order)), const(x_backward(grid, group)), *backs)
    return result[None]


def solution(mesh):
    return jax.shard_map(
        local,
        mesh=mesh,
        in_specs=(P("pool", None, None, "fft", None), P(), P()),
        out_specs=P("pool", None, None, "fft", None),
        check_vma=False,
    )
```

time: 178 us -> 144 us (0.81)
  Pallas kernels: 50 us -> 120 us
  waiting for transfers between devices: 63.8 us -> 0 us
  blocking collectives: 34.8 us -> 0 us
  starting transfers between devices: 6.91 us -> 0 us
  other arithmetic: 6.67 us -> 9.58 us
    pallas_call x3 -> x2, Pallas kernels: 50 us -> 120 us  [the longest x1 105 us: local(): pl.pallas_call(functools.partial(exchange_kernel, grid, group, margin, po...]
    ppermute x1 -> x0, waiting for transfers between devices: 42.9 us -> none  [local(): lax.ppermute(orbitals, 'pool', [(p, (p + 1) % pool) for p in range(pool)])]
    all_to_all x1 -> x0, blocking collectives: 34.8 us -> none  [local(): lax.all_to_all(returned, 'fft', split_axis=0, concat_axis=0, tiled=True)]
    all_to_all x1 -> x0, waiting for transfers between devices: 20.9 us -> none  [local(): lax.all_to_all(sent, 'fft', split_axis=0, concat_axis=0, tiled=True)]
    all_to_all x1 -> x0, starting transfers between devices: 3.86 us -> none  [local(): lax.all_to_all(sent, 'fft', split_axis=0, concat_axis=0, tiled=True)]
    ppermute x1 -> x0, starting transfers between devices: 3.05 us -> none  [local(): lax.ppermute(orbitals, 'pool', [(p, (p + 1) % pool) for p in range(pool)])]
    ppermute x1 -> x0, local copies, waits for them, and re-layouts: 1.83 us -> none  [local(): lax.ppermute(orbitals, 'pool', [(p, (p + 1) % pool) for p in range(pool)])]
  transfers between devices with their start and end apart: 2 -> 0, of which waited for: 2 -> 0; matrix products, arithmetic and copies ran while one was open for 8% -> 0% of each run, Pallas kernels for 0% -> 0%
where the time goes in v2:
time: 144 us
  Pallas kernels  120 us (83%)
  local copies, waits for them, and re-layouts  10.9 us (8%)
  other arithmetic  9.58 us (7%)
  matrix products  3.37 us (2%)
    pallas_call x1, Pallas kernels, local(): pl.pallas_call(functools.partial(exchange_kernel, grid, group, margin, po...  105 us
    pallas_call x1, Pallas kernels, local(): pl.pallas_call(functools.partial(backward_kernel, grid, group), grid=(gri...  14.6 us
    unnamed x13, local copies, waits for them, and re-layouts  5.11 us
    broadcast_in_dim x1, local copies, waits for them, and re-layouts, local(): return result[None]  5.1 us
    select_n x1, other arithmetic, weight_table(): return jnp.where(inside, weights, 0.0)  4.04 us
    dot_general x1, matrix products, weight_table(): lax.dot_general(at_y, at_x, (((1,), (1,)), ((), ())), preferred_element_t...  3.37 us

profile of v2, /device:TPU:0, one launch (start us, length us, event | category | flops | bytes accessed | tf_op | source)
XLA Modules:
  0.0 143.5 jit_solution(16175684006939743173)
XLA Ops:
  0.0 0.0 copy-start.5
  0.0 0.9 select_reduce_fusion
  0.9 0.7 fusion.18
  1.6 0.7 add_multiply_fusion.1
  2.3 0.7 add_multiply_fusion.2
  3.0 1.2 add_multiply_fusion
  4.2 0.1 broadcast_add_fusion
  4.3 0.8 broadcast_add_fusion.1
  5.0 0.9 fusion.13
  6.0 0.3 fusion.25
  6.2 3.4 %fusion.6 = pred[20,256]{1,0:T(8,128)(4,1)S(1)} fusion(s32[16000]{0:T(1024)S(1)} %get-tuple-element.16, s32[256]{0:T(256)} %constant.95.clone, pred[20,16000]{1,0:T(8,128)(4,1)S(1)} %fusion.25), kind=kOutput, calls=%fused_computation.9 | convolution fusion | flops 167941120 | bytes 390144 | tf_op jit(solution)/shard_map/dot_general | solution.py:346
  9.6 0.0 copy-done.5
  9.6 1.8 %copy.14 = bf16[1,2,1,20,25600]{4,3,1,2,0:T(8,128)(2,1)} copy(bf16[1,2,1,20,25600]{4,1,3,2,0:T(2,128)(2,1)S(1)} %copy-done.5) | data formatting | bytes 4096000 | tf_op args[0]
  11.4 4.0 %multiply_select_fusion.refs_1_ = f32[20,160,256]{2,1,0:T(8,128)} fusion(f32[20,256]{1,0:T(8,128)S(1)} %broadcast_add_fusion, f32[160]{0:T(256)S(1)} %add_multiply_fusion.1, s32[160]{0:T(256)S(1)} %fusion.16, s32[20,256]{1,0:T(8,128)S(1)} %broadcast_add_fusion.1, pred[20,256]{1,0:T(8,128)(4,1)S(1)} %fusion.6), kind=kLoop, calls=%fused_computation.4 | loop fusion | flops 9830400 | bytes 3324160 | tf_op jit(solution)/shard_map/jit(_where)/select_n | solution.py:358
  15.5 0.0 copy-start
  15.5 0.0 copy-start.4
  15.5 105.0 %shard_map.100 = (bf16[2,1,20,25600]{3,2,1,0:T(8,128)(2,1)}, bf16[8,400,128]{2,1,0:T(8,128)(2,1)}, bf16[8,400,128]{2,1,0:T(8,128)(2,1)}, bf16[8,208,128]{2,1,0:T(8,128)(2,1)}) custom-call(bf16[2,1,20,25600]{3,2,1,0:T(8,128)(2,1)} %bitcast.8, f32[20,160,256]{2,1,0:T(8,128)} %multiply_select_fusion.refs_1_, bf16[2,352,384]{2,1,0:T(8,128)(2,1)} %constant.96.clone.refs_2_, ...), custom_call_target="tpu_custom_call" | custom-call | tf_op jit(solution)/shard_map/pallas_call | solution.py:378
  120.5 0.0 copy-done
  120.5 0.0 copy-done.4
  120.5 0.0 copy-start.1
  120.5 1.1 copy-done.1
  121.6 0.0 copy-start.2
  121.6 1.1 copy-done.2
  122.8 0.0 copy-start.3
  122.8 1.0 copy-done.3
  123.8 14.6 %shard_map.101 = bf16[2,1,20,25600]{3,2,1,0:T(8,128)(2,1)} custom-call(bf16[2,1,20,25600]{3,2,1,0:T(8,128)(2,1)} %get-tuple-element.9.refs_0_, bf16[160,384]{1,0:T(8,128)(2,1)S(1)} %copy-done.4, bf16[4,384,512]{2,1,0:T(8,128)(2,1)S(1)} %copy-done, bf16[8,400,128]{2,1,0:T(8,128)(2,1)S(1)} %copy-done.1, bf16[8,400,128]{2,1,0:T(8,128)(2,1)S(1)} %copy-done.2, ...), custom_call_target="tpu_custom_call" | custom-call | tf_op jit(solution)/shard_map/pallas_call | solution.py:402
  138.4 5.1 %copy.12 = bf16[1,2,1,20,25600]{4,1,3,2,0:T(2,128)(2,1)} copy(bf16[1,2,1,20,25600]{4,3,1,2,0:T(8,128)(2,1)} %bitcast.9) | data formatting | bytes 4096000 | tf_op jit(solution)/shard_map/broadcast_in_dim | solution.py:411
  (4 shorter events, 0.0 us)
Async XLA Ops:
  0.0 9.6 %copy-start.5 = (bf16[1,2,1,20,25600]{4,1,3,2,0:T(2,128)(2,1)S(1)}, bf16[1,2,1,20,25600]{4,1,3,2,0:T(2,128)(2,1)}, u32[]{:S(2)}) copy-start(bf16[1,2,1,20,25600]{4,1,3,2,0:T(2,128)(2,1)} %param.10) | copy-start | bytes 6144004
  15.5 105.0 %copy-start = (bf16[4,384,512]{2,1,0:T(8,128)(2,1)S(1)}, bf16[4,384,512]{2,1,0:T(8,128)(2,1)}, u32[]{:S(2)}) copy-start(bf16[4,384,512]{2,1,0:T(8,128)(2,1)} %constant.101.clone.refs_2_) | copy-start | bytes 4718596
  15.5 105.0 %copy-start.4 = (bf16[160,384]{1,0:T(8,128)(2,1)S(1)}, bf16[160,384]{1,0:T(8,128)(2,1)}, u32[]{:S(2)}) copy-start(bf16[160,384]{1,0:T(8,128)(2,1)} %constant.100.clone.refs_1_) | copy-start | bytes 368644
  120.5 1.1 copy-start.1
  121.6 1.1 copy-start.2
  122.8 1.0 copy-start.3

commit v3 on v2

--- a/solution.py
+++ b/solution.py
@@ -147,7 +147,8 @@
 
 
 def exchange_kernel(grid, group, margin, pools, *refs):
-    own, weights, wx, fy, fz, bz, rec, refs = *refs[:7], refs[7:]
+    own, slots, kx_rows, kx_lanes, q, wx, fy, fz, bz, rec, refs = *refs[:10], refs[10:]
+    weights, present, refs = refs[-2], refs[-1], refs[:-2]
     planes = rec.shape[2]
     parts = cuts(planes)
     n = len(parts)
@@ -183,6 +184,7 @@
         )
         moves[c].start()
     fetch.wait()
+    fill_weights(grid, planes, me * planes, slots, kx_rows, kx_lanes, q, present, weights)
 
     def post(c, source, landing, send_sem, recv_sem):
         copies = []
@@ -324,38 +326,50 @@
     return jnp.where(frequency >= grid // 2, frequency - grid, frequency)
 
 
-def weight_table(stick_map, kpoint_grid, grid, planes):
-    pool_count, pool_rank = lax.axis_size("pool"), lax.axis_index("pool")
-    rows = jnp.arange(pool_count, dtype=jnp.int32)
-    earlier = (pool_rank + pool_count - 1) % pool_count
-    current = jnp.sum(jnp.where((rows == pool_rank)[:, None], kpoint_grid, 0), axis=0)
-    previous = jnp.sum(jnp.where((rows == earlier)[:, None], kpoint_grid, 0), axis=0)
-    shift = (current - previous).astype(F32) / KMESH
+def spectral_kx(grid):
     low, high = lane_order(grid)
     order = np.full((2 * LANES,), -1, np.int32)
     order[:LANES] = low
     order[LANES : LANES + high.size] = high
     order[LANES + LANES // 2 : LANES + LANES // 2 + high.size] = high
-    kx = jnp.asarray(order)
-    ky = lax.axis_index("fft") * planes + jnp.arange(planes, dtype=jnp.int32)
-    live = stick_map >= 0
-    slot_y = jnp.where(live, stick_map // grid, -2)
-    slot_x = jnp.where(live, stick_map % grid, -2)
-    at_y = (ky[:, None] == slot_y[None, :]).astype(BF)
-    at_x = (kx[:, None] == slot_x[None, :]).astype(BF)
-    present = lax.dot_general(at_y, at_x, (((1,), (1,)), ((), ())), preferred_element_type=F32) > 0.5
-    fx, fy = signed(kx, grid), signed(ky, grid)
-    fz = signed(jnp.arange(grid, dtype=jnp.int32), grid)
+    return order
+
+
+def fill_weights(grid, planes, first_ky, slots, kx_rows, kx_lanes, shift, present, weights):
+    tall = present.shape[0]
+    width = slots.shape[1] // 5
+    present[...] = jnp.zeros(present.shape, F32)
+    ky = first_ky + lax.broadcasted_iota(jnp.int32, (tall, width), 0)
+
+    def find(i, _):
+        lanes = pl.ds(pl.multiple_of(i * width, LANES), width)
+        at_y = jnp.where(ky == slots[0:1, lanes], 1.0, 0.0).astype(BF)
+        at_x = jnp.where(kx_rows[...] == slots[1:2, lanes], 1.0, 0.0).astype(BF)
+        present[...] += lax.dot_general(at_y, at_x, (((1,), (1,)), ((), ())), preferred_element_type=F32)
+        return 0
+
+    lax.fori_loop(0, 5, find, 0)
+    shape = (grid, 2 * LANES)
+    fx = signed(jnp.broadcast_to(kx_lanes[...], shape), grid)
+    fz = signed(lax.broadcasted_iota(jnp.int32, shape, 0), grid)
+    wx = fx.astype(F32) + shift[0:1, :]
+    wz = fz.astype(F32) + shift[2:3, :]
+    flat = fx * fx + fz * fz
+    partial = wz * wz + wx * wx
     radius = grid // 2
-    flat = fx[None, :] * fx[None, :] + fy[:, None] * fy[:, None]
-    inside = (flat[:, None, :] + (fz * fz)[None, :, None] <= radius * radius) & present[:, None, :]
-    wx, wy, wz = [f.astype(F32) + q for f, q in ((fx, shift[0]), (fy, shift[1]), (fz, shift[2]))]
-    square = (wz * wz)[None, :, None] + ((wx * wx)[None, :] + (wy * wy)[:, None])[:, None, :]
-    square = jnp.where(inside, square, 1.0)
     cell = SPACING_BOHR * grid
-    exponent = math.pi * math.pi * square / (cell * cell * SCREENING * SCREENING)
-    weights = cell * cell / math.pi * -jnp.expm1(-exponent) / square / float(grid) ** 3
-    return jnp.where(inside, weights, 0.0)
+    rate = math.pi * math.pi / (cell * cell * SCREENING * SCREENING)
+    scale = cell * cell / math.pi / float(grid) ** 3
+
+    def fill(k, _):
+        fy = signed(first_ky + k, grid)
+        wy = fy.astype(F32) + shift[1:2, :]
+        inside = (flat + fy * fy <= radius * radius) & (present[pl.ds(k, 1), :] > 0.5)
+        square = jnp.where(inside, partial + wy * wy, 1.0)
+        weights[k] = jnp.where(inside, scale * (1.0 - jnp.exp(-rate * square)) / square, 0.0)
+        return 0
+
+    lax.fori_loop(0, planes, fill, 0)
 
 
 def local(orbitals, stick_map, kpoint_grid):
@@ -373,12 +387,21 @@
     biggest = max(size for _, size in parts)
 
     own = orbitals[0]
-    weights = weight_table(stick_map, kpoint_grid, grid, planes)
+    pool_rank = lax.axis_index("pool")
+    ranks = jnp.arange(pools, dtype=jnp.int32)
+    earlier = (pool_rank + pools - 1) % pools
+    sign = (ranks == pool_rank).astype(jnp.int32) - (ranks == earlier).astype(jnp.int32)
+    q = jnp.sum(sign[:, None] * kpoint_grid, axis=0).astype(F32) / KMESH
+    q = jnp.broadcast_to(q[:, None], (3, 2 * LANES))
+    live = stick_map >= 0
+    slots = jnp.stack([jnp.where(live, stick_map // grid, -2), jnp.where(live, stick_map % grid, -2)])
+    slots = jnp.pad(slots, ((0, 0), (0, -slots.shape[1] % (5 * LANES))), constant_values=-2)
+    kx = spectral_kx(grid)
     wx, margin = x_forward(grid, group)
     rec, *backs = pl.pallas_call(
         functools.partial(exchange_kernel, grid, group, margin, pools),
         out_shape=[jax.ShapeDtypeStruct(own.shape, BF)] + [jax.ShapeDtypeStruct(p, BF) for p in parcels],
-        in_specs=[pl.BlockSpec(memory_space=pl.ANY)] + [vmem] * 5,
+        in_specs=[pl.BlockSpec(memory_space=pl.ANY)] + [vmem] * 8,
         out_specs=[vmem] * (1 + n),
         scratch_shapes=[pltpu.VMEM(p, BF) for p in parcels]
         + [pltpu.VMEM(p, BF) for p in parcels]
@@ -392,9 +415,10 @@
             pltpu.SemaphoreType.DMA((n,)),
             pltpu.SemaphoreType.DMA((n,)),
         ]
-        + [pltpu.SemaphoreType.DMA((n, devices - 1)) for _ in range(4)],
+        + [pltpu.SemaphoreType.DMA((n, devices - 1)) for _ in range(4)]
+        + [pltpu.VMEM((planes, grid, 2 * LANES), F32), pltpu.VMEM((up(planes, 8), 2 * LANES), F32)],
         compiler_params=pltpu.CompilerParams(vmem_limit_bytes=60 * 2**20, collective_id=0, has_side_effects=True),
-    )(own, weights, const(wx), const(left(grid, -1.0)), const(left_cut(grid, -1.0, devices, planes)), const(left(grid, 1.0)))
+    )(own, slots, jnp.asarray(kx[:, None]), jnp.asarray(kx[None, :]), q, const(wx), const(left(grid, -1.0)), const(left_cut(grid, -1.0, devices, planes)), const(left(grid, 1.0)))
 
     y_order = np.arange(grid).reshape(grid // group, group).T.reshape(-1)
     step = 4

time: 144 us -> 134 us (0.931)
  other arithmetic: 9.58 us -> 2.44 us
  matrix products: 3.37 us -> 0 us
  local copies, waits for them, and re-layouts: 10.9 us -> 12.5 us
    select_n x2 -> x1, other arithmetic: 4.95 us -> 0.91 us  [local(): jnp.where(live, stick_map // grid, -2)]
    dot_general x1 -> x0, matrix products: 3.37 us -> none  [weight_table(): lax.dot_general(at_y, at_x, (((1,), (1,)), ((), ())), preferred_element_t...]
    mul x4 -> x0, other arithmetic: 2.59 us -> none  [the longest x1 1.24 us: weight_table(): wx * wx]
    unnamed x13 -> x11, local copies, waits for them, and re-layouts: 5.11 us -> 6.66 us
where the time goes in v3:
time: 134 us
  Pallas kernels  119 us (89%)
  local copies, waits for them, and re-layouts  12.5 us (9%)
  other arithmetic  2.44 us (2%)
    pallas_call x1, Pallas kernels, local(): pl.pallas_call(functools.partial(exchange_kernel, grid, group, margin, po...  104 us
    pallas_call x1, Pallas kernels, local(): pl.pallas_call(functools.partial(backward_kernel, grid, group), grid=(gri...  14.7 us
    unnamed x11, local copies, waits for them, and re-layouts  6.66 us
    broadcast_in_dim x1, local copies, waits for them, and re-layouts, local(): return result[None]  5.1 us

profile of v3, /device:TPU:0, one launch (start us, length us, event | category | flops | bytes accessed | tf_op | source)
XLA Modules:
  0.0 133.6 jit_solution(6927096667663904723)
XLA Ops:
  0.0 0.8 multiply_reduce_fusion
  0.8 0.7 broadcast_in_dim.16.refs_4_
  1.4 0.9 fusion
  2.5 0.8 pad_add_fusion.refs_1_
  3.2 3.4 %copy.15 = bf16[1,2,1,20,25600]{4,3,1,2,0:T(8,128)(2,1)} copy(bf16[1,2,1,20,25600]{4,1,3,2,0:T(2,128)(2,1)} %param.11) | data formatting | bytes 4096000 | tf_op args[0]
  6.6 0.0 copy-start
  6.6 0.0 copy-start.4
  6.6 103.9 %shard_map.109 = (bf16[2,1,20,25600]{3,2,1,0:T(8,128)(2,1)}, bf16[8,400,128]{2,1,0:T(8,128)(2,1)}, bf16[8,400,128]{2,1,0:T(8,128)(2,1)}, bf16[8,208,128]{2,1,0:T(8,128)(2,1)}) custom-call(bf16[2,1,20,25600]{3,2,1,0:T(8,128)(2,1)} %bitcast.5, s32[2,16000]{1,0:T(2,128)} %pad_add_fusion.refs_1_, s32[256,1]{1,0:T(8,128)} %constant.63.clone.refs_2_, ...), custom_call_target="tpu_custom_call" | custom-call | tf_op jit(solution)/shard_map/pallas_call | solution.py:401
  110.5 0.0 copy-done
  110.5 0.0 copy-done.4
  110.5 0.0 copy-start.1
  110.5 1.1 copy-done.1
  111.7 0.0 copy-start.2
  111.7 1.1 copy-done.2
  112.8 0.0 copy-start.3
  112.8 1.0 copy-done.3
  113.8 14.7 %shard_map.110 = bf16[2,1,20,25600]{3,2,1,0:T(8,128)(2,1)} custom-call(bf16[2,1,20,25600]{3,2,1,0:T(8,128)(2,1)} %get-tuple-element.9.refs_0_, bf16[160,384]{1,0:T(8,128)(2,1)S(1)} %copy-done.4, bf16[4,384,512]{2,1,0:T(8,128)(2,1)S(1)} %copy-done, bf16[8,400,128]{2,1,0:T(8,128)(2,1)S(1)} %copy-done.1, bf16[8,400,128]{2,1,0:T(8,128)(2,1)S(1)} %copy-done.2, ...), custom_call_target="tpu_custom_call" | custom-call | tf_op jit(solution)/shard_map/pallas_call | solution.py:426
  128.5 5.1 %copy.13 = bf16[1,2,1,20,25600]{4,1,3,2,0:T(2,128)(2,1)} copy(bf16[1,2,1,20,25600]{4,3,1,2,0:T(8,128)(2,1)} %bitcast.4) | data formatting | bytes 4096000 | tf_op jit(solution)/shard_map/broadcast_in_dim | solution.py:435
  (4 shorter events, 0.1 us)
Async XLA Ops:
  6.6 103.9 %copy-start = (bf16[4,384,512]{2,1,0:T(8,128)(2,1)S(1)}, bf16[4,384,512]{2,1,0:T(8,128)(2,1)}, u32[]{:S(2)}) copy-start(bf16[4,384,512]{2,1,0:T(8,128)(2,1)} %constant.70.clone.refs_2_) | copy-start | bytes 4718596
  6.6 103.9 %copy-start.4 = (bf16[160,384]{1,0:T(8,128)(2,1)S(1)}, bf16[160,384]{1,0:T(8,128)(2,1)}, u32[]{:S(2)}) copy-start(bf16[160,384]{1,0:T(8,128)(2,1)} %constant.69.clone.refs_1_) | copy-start | bytes 368644
  110.5 1.1 copy-start.1
  111.7 1.1 copy-start.2
  112.8 1.0 copy-start.3
